TPU v7x, 32 devices: a whole 2x2x4 slice. The times are simulated.
32 devices in a mesh: view: 4 (over x, core), gauss: 8 (over z, y).
Axes of the slice: x: 2, y: 2, z: 4, core: 2. Of those that a mesh axis runs over, the one named last changes fastest.
Arguments:
- means: float32 [3, 131072], P(None, 'gauss'), may hold values from -1 to 1
- scales: float32 [3, 131072], P(None, 'gauss'), may hold values from 0.05 to 0.6
- quats: float32 [4, 131072], P(None, 'gauss'), may hold values from -6 to 6
- attrs: float32 [49, 131072], P(None, 'gauss'), may hold values from -6 to 6
- grad_screen: float32 [16, 2, 131072], P('view', None, 'gauss'), may hold values from -6 to 6
- visible: int32 [16, 131072], P('view', 'gauss'), may hold values 0 or 1
- clone_mask: int32 [131072], P('gauss'), may hold values from 0 to 1, as said below
- rotation: float32 [16, 3, 3], P('view'), may hold values from -3.5 to 3.5
- shift: float32 [16, 3], P('view'), may hold values from 2 to 5
- focal: float32 [16], P('view'), may hold values from 1 to 4
Outputs:
- peak_stats: float32 [2, 131072], P(None, 'gauss')
- clones: float32 [61, 131072], P(None, 'gauss')
- clone_total: int32 [], replicated
Inputs may be any that keep to these rules, and one draw needn't show every extreme that they name: `clone_mask`: in every draw some shard of 16384 consecutive Gaussians has all of them marked.
All inputs are finite; a program needn't handle non-finite values. No bound on the sum of `visible` on one device may be relied on, other than what follows from the above.
Results may differ from a plain program's by a relative error of at most 0.0003.
Values sent between devices are 32-bit elements; how exact they have to be, the bound alone decides.
A program may use at most 128 MiB of HBM per device.

v0:
```python
import jax
import jax.numpy as jnp
from jax import lax
from jax.sharding import PartitionSpec as P

G_DEV = 16384


def entering(value, axis, join, neutral):
    count, mine = (lax.axis_size(axis), lax.axis_index(axis))
    pieces = lax.all_gather(value, axis)
    running = jnp.full_like(value, 0) + jnp.asarray(neutral, value.dtype)

    def step(position, running):
        longer = join(running, pieces[position])
        return jnp.where(position < mine, longer, running)

    return lax.fori_loop(0, count - 1, step, running)


def quat_factor(scales, quats):
    inv = 1.0 / jnp.sqrt(jnp.sum(quats * quats, axis=0) + 0.25)
    w, x, y, z = (quats[0] * inv, quats[1] * inv, quats[2] * inv, quats[3] * inv)
    rq = [
        [1 - 2 * (y * y + z * z), 2 * (x * y - w * z), 2 * (x * z + w * y)],
        [2 * (x * y + w * z), 1 - 2 * (x * x + z * z), 2 * (y * z - w * x)],
        [2 * (x * z - w * y), 2 * (y * z + w * x), 1 - 2 * (x * x + y * y)],
    ]
    return [[rq[i][j] * scales[j] for j in range(3)] for i in range(3)]


def view_stats(means, factor, grad, seen, rot, trans, focal_v):
    point = [
        rot[i, 0] * means[0] + rot[i, 1] * means[1] + rot[i, 2] * means[2] + trans[i]
        for i in range(3)
    ]
    depth = jnp.maximum(point[2], 1.0)
    j00 = focal_v / depth
    j02 = -focal_v * point[0] / (depth * depth)
    j12 = -focal_v * point[1] / (depth * depth)
    first = [j00 * rot[0, j] + j02 * rot[2, j] for j in range(3)]
    second = [j00 * rot[1, j] + j12 * rot[2, j] for j in range(3)]
    prow = [sum((first[j] * factor[j][k] for j in range(3))) for k in range(3)]
    qrow = [sum((second[j] * factor[j][k] for j in range(3))) for k in range(3)]
    a_val = prow[0] ** 2 + prow[1] ** 2 + prow[2] ** 2 + 0.3
    c_val = qrow[0] ** 2 + qrow[1] ** 2 + qrow[2] ** 2 + 0.3
    b_val = prow[0] * qrow[0] + prow[1] * qrow[1] + prow[2] * qrow[2]
    half = 0.5 * (a_val - c_val)
    lam = 0.5 * (a_val + c_val) + jnp.sqrt(half * half + b_val * b_val + 0.01)
    seenf = seen.astype(jnp.float32)
    radius = 3.0 * jnp.sqrt(lam) * seenf
    gnorm = jnp.sqrt(grad[0] * grad[0] + grad[1] * grad[1]) * seenf
    return (gnorm, radius)


def add_ints(earlier, later):
    return earlier + later


def body(means, scales, quats, attrs, grad_screen, visible, clone_mask, rotation, shift, focal):
    factor = quat_factor(scales, quats)
    gmax = jnp.zeros(means.shape[1], jnp.float32)
    rmax = jnp.zeros(means.shape[1], jnp.float32)
    for v in range(grad_screen.shape[0]):
        gnorm, radius = view_stats(
            means, factor, grad_screen[v], visible[v], rotation[v], shift[v], focal[v]
        )
        gmax = jnp.maximum(gmax, gnorm)
        rmax = jnp.maximum(rmax, radius)
    gmax, rmax = lax.pmax((gmax, rmax), "view")
    peak = jnp.stack([gmax, rmax])
    rows = jnp.concatenate([means, scales, quats, attrs, peak], axis=0)
    feat_rows = rows.shape[0]
    shards = lax.axis_size("gauss")
    cap_blk = G_DEV // 128
    count = jnp.sum(clone_mask)
    blocks = (count + 127) // 128
    offset = entering(blocks, "gauss", add_ints, jnp.int32(0))
    summed = lax.psum(count.astype(jnp.float32), "gauss")
    total = summed.astype(jnp.int32)
    rank = jnp.cumsum(clone_mask) - 1
    where_to = jnp.where(clone_mask == 1, rank, cap_blk * 128)
    packed = (
        jnp.zeros((feat_rows, cap_blk * 128), jnp.float32).at[:, where_to].set(rows, mode="drop")
    )
    packed = packed.reshape(feat_rows, cap_blk, 128)
    per = (cap_blk + shards - 1) // shards
    target = jnp.arange(shards, dtype=jnp.int32)[:, None]
    within = jnp.arange(per, dtype=jnp.int32)[None, :]
    local_blk = (target - offset) % shards + within * shards
    valid = local_blk < blocks
    picked = jnp.minimum(local_blk, cap_blk - 1).reshape(-1)
    outgoing = packed[:, picked, :] * valid.reshape(1, -1, 1).astype(jnp.float32)
    outgoing = outgoing.reshape(feat_rows, shards, per, 128)
    slot_ids = (
        jnp.where(valid, (offset + local_blk) // shards, cap_blk)
        .astype(jnp.int32)
        .reshape(1, shards, per)
    )
    width = 128 // lax.axis_size("view")
    start = lax.axis_index("view") * width
    portion = lax.dynamic_slice_in_dim(outgoing, start, width, 3)
    arrived, slots_in = (
        lax.all_to_all(portion, "gauss", split_axis=1, concat_axis=1, tiled=True),
        lax.all_to_all(slot_ids, "gauss", split_axis=1, concat_axis=1, tiled=True),
    )
    arrived = arrived.reshape(feat_rows, shards * per, width)
    partial_place = (
        jnp.zeros((feat_rows, cap_blk, width), jnp.float32)
        .at[:, slots_in.reshape(-1)]
        .set(arrived, mode="drop")
    )
    placed = lax.all_gather(partial_place, "view", axis=2, tiled=True)
    clones = placed.reshape(feat_rows, cap_blk * 128)
    return (peak, clones, total)


def solution(mesh):
    return jax.shard_map(
        body,
        mesh=mesh,
        in_specs=(
            P(None, "gauss"),
            P(None, "gauss"),
            P(None, "gauss"),
            P(None, "gauss"),
            P("view", None, "gauss"),
            P("view", "gauss"),
            P("gauss"),
            P("view", None, None),
            P("view", None),
            P("view"),
        ),
        out_specs=(P(None, "gauss"), P(None, "gauss"), P()),
        check_vma=False,
    )
```

profile of v0, /device:TPU:0, one launch (start us, length us, event | category | flops | bytes accessed | tf_op | source)
XLA Modules:
  0.0 360.1 jit_solution(10346555730215635345)
XLA Ops:
  13.1 13.1 %all-reduce = s32[8]{0:T(128)S(1)} all-reduce(s32[8]{0:T(128)S(1)} %dynamic-update-slice), channel_id=1, replica_groups=mesh['view'=4,'gauss'=8] {'gauss'}, use_global_device_ids=true, to_apply=%add | all-reduce | flops 8 | bytes 64
  26.2 8.9 %while.13 = (s32[]{:T(128)}, s32[]{:T(128)}, s32[]{:T(128)}, s32[8]{0:T(128)S(1)}, s32[]{:T(128)}) while((s32[]{:T(128)}, s32[]{:T(128)}, s32[]{:T(128)}, s32[8]{0:T(128)S(1)}, s32[]{:T(128)}) %tuple.130), condition=%wide.region_5.6_spmd, body=%wide.region_4.5_spmd.sunk | while | flops 5 | bytes 107 | solution.py:18
  35.8 3.3 all-to-all-start
  39.2 1.7 fusion.6
  43.6 1.8 fusion.10
  47.5 7.4 %multiply_add_fusion.23 = (f32[1,16384]{1,0:T(1,128)S(1)}, f32[1,16384]{1,0:T(1,128)S(1)}, f32[1,16384]{1,0:T(1,128)S(1)}, f32[1,16384]{1,0:T(1,128)S(1)}) fusion(f32[]{:T(128)} %bitcast.15, f32[]{:T(128)} %bitcast.11, f32[]{:T(128)} %bitcast.18, f32[3,16384]{1,0:T(4,128)} %param.12, f32[]{:T(128)} %bitcast.17, f32[]{:T(128)} %bitcast.16, f32[]{:T(128)S(6)} %neg.16, ...), kind=kLoop, calls=%fused_computation.34 | loop fusion | flops 327680 | bytes 458792 | tf_op jit(solution)/shard_map/add | solution.py:41
  54.9 7.5 %multiply_add_fusion.22 = (f32[1,16384]{1,0:T(1,128)S(1)}, f32[1,16384]{1,0:T(1,128)S(1)}, f32[1,16384]{1,0:T(1,128)S(1)}, f32[1,16384]{1,0:T(1,128)S(1)}) fusion(f32[1,16384]{1,0:T(1,128)S(1)} %get-tuple-element.103, f32[1,16384]{1,0:T(1,128)S(1)} %get-tuple-element.104, f32[]{:T(128)} %bitcast.16, f32[]{:T(128)} %bitcast.12, f32[]{:T(128)} %bitcast.13, ...), kind=kLoop, calls=%fused_computation.33 | loop fusion | flops 294912 | bytes 655400 | tf_op jit(solution)/shard_map/add | solution.py:41
  62.4 2.7 multiply_add_fusion.19
  66.4 7.5 %multiply_add_fusion.17 = (f32[1,16384]{1,0:T(1,128)S(1)}, f32[1,16384]{1,0:T(1,128)S(1)}, f32[1,16384]{1,0:T(1,128)S(1)}, f32[1,16384]{1,0:T(1,128)S(1)}) fusion(f32[]{:T(128)} %bitcast.41, f32[]{:T(128)} %bitcast.37, f32[]{:T(128)} %bitcast.44, f32[3,16384]{1,0:T(4,128)} %param.12, f32[]{:T(128)} %bitcast.43, f32[]{:T(128)} %bitcast.42, f32[]{:T(128)S(6)} %neg.17, ...), kind=kLoop, calls=%fused_computation.28 | loop fusion | flops 327680 | bytes 458792 | tf_op jit(solution)/shard_map/add | solution.py:41
  73.8 6.1 %multiply_add_fusion.16 = (f32[1,16384]{1,0:T(1,128)S(1)}, f32[1,16384]{1,0:T(1,128)S(1)}, f32[1,16384]{1,0:T(1,128)S(1)}, f32[1,16384]{1,0:T(1,128)S(1)}) fusion(f32[1,16384]{1,0:T(1,128)S(1)} %get-tuple-element.109, f32[1,16384]{1,0:T(1,128)S(1)} %get-tuple-element.110, f32[]{:T(128)} %bitcast.42, f32[]{:T(128)} %bitcast.38, f32[]{:T(128)} %bitcast.39, ...), kind=kLoop, calls=%fused_computation.27 | loop fusion | flops 294912 | bytes 655400 | tf_op jit(solution)/shard_map/add | solution.py:41
  79.9 2.7 multiply_add_fusion.13
  84.1 6.3 %multiply_add_fusion.11 = (f32[1,16384]{1,0:T(1,128)S(1)}, f32[1,16384]{1,0:T(1,128)S(1)}, f32[1,16384]{1,0:T(1,128)S(1)}, f32[1,16384]{1,0:T(1,128)S(1)}) fusion(f32[]{:T(128)} %bitcast.60, f32[]{:T(128)} %bitcast.56, f32[]{:T(128)} %bitcast.63, f32[3,16384]{1,0:T(4,128)S(1)} %copy-done.1, f32[]{:T(128)} %bitcast.62, f32[]{:T(128)} %bitcast.61, ...), kind=kLoop, calls=%fused_computation.22 | loop fusion | flops 327680 | bytes 458792 | tf_op jit(solution)/shard_map/add | solution.py:41
  90.4 6.1 %multiply_add_fusion.10 = (f32[1,16384]{1,0:T(1,128)S(1)}, f32[1,16384]{1,0:T(1,128)S(1)}, f32[1,16384]{1,0:T(1,128)S(1)}, f32[1,16384]{1,0:T(1,128)S(1)}) fusion(f32[1,16384]{1,0:T(1,128)S(1)} %get-tuple-element.115, f32[1,16384]{1,0:T(1,128)S(1)} %get-tuple-element.116, f32[]{:T(128)} %bitcast.61, f32[]{:T(128)} %bitcast.57, f32[]{:T(128)} %bitcast.58, ...), kind=kLoop, calls=%fused_computation.21 | loop fusion | flops 294912 | bytes 655400 | tf_op jit(solution)/shard_map/add | solution.py:41
  96.4 2.6 multiply_add_fusion.7
  100.3 6.1 %multiply_add_fusion.5 = (f32[1,16384]{1,0:T(1,128)S(1)}, f32[1,16384]{1,0:T(1,128)S(1)}, f32[1,16384]{1,0:T(1,128)S(1)}, f32[1,16384]{1,0:T(1,128)S(1)}) fusion(f32[]{:T(128)} %bitcast.79, f32[]{:T(128)} %bitcast.75, f32[]{:T(128)} %bitcast.82, f32[3,16384]{1,0:T(4,128)S(1)} %copy-done.1, f32[]{:T(128)} %bitcast.81, f32[]{:T(128)} %bitcast.80, f32[]{:T(128)S(6)} %neg.19, ...), kind=kLoop, calls=%fused_computation.16 | loop fusion | flops 327680 | bytes 458792 | tf_op jit(solution)/shard_map/add | solution.py:41
  106.3 6.2 %multiply_add_fusion.4 = (f32[1,16384]{1,0:T(1,128)S(1)}, f32[1,16384]{1,0:T(1,128)S(1)}, f32[1,16384]{1,0:T(1,128)S(1)}, f32[1,16384]{1,0:T(1,128)S(1)}) fusion(f32[1,16384]{1,0:T(1,128)S(1)} %get-tuple-element.121, f32[1,16384]{1,0:T(1,128)S(1)} %get-tuple-element.122, f32[]{:T(128)} %bitcast.80, f32[]{:T(128)} %bitcast.76, f32[]{:T(128)} %bitcast.77, ...), kind=kLoop, calls=%fused_computation.15 | loop fusion | flops 294912 | bytes 655400 | tf_op jit(solution)/shard_map/add | solution.py:41
  112.5 2.6 multiply_add_fusion.1
  118.6 33.1 %all-reduce.4.cloned.1.call-done = (f32[1,16384]{1,0:T(1,128)}, f32[1,16384]{1,0:T(1,128)}) async-done(((f32[1,16384]{1,0:T(1,128)}, f32[1,16384]{1,0:T(1,128)}), (f32[1,16384]{1,0:T(1,128)}, f32[1,16384]{1,0:T(1,128)})) %all-reduce.4.cloned.1.call-update) | async-done | bytes 131088 | tf_op jit(solution)/shard_map/pmax | solution.py:70
  151.7 21.6 %concatenate.4 = f32[61,16384]{1,0:T(8,128)} concatenate(f32[3,16384]{1,0:T(4,128)S(1)} %copy-done.1, f32[3,16384]{1,0:T(4,128)S(1)} %copy-done.3, f32[4,16384]{1,0:T(4,128)S(1)} %copy-done.2, f32[49,16384]{1,0:T(8,128)} %param.15, f32[1,16384]{1,0:T(1,128)} %get-tuple-element.101, f32[1,16384]{1,0:T(1,128)} %get-tuple-element.100), dimensions={0} | concatenate | bytes 7995392 | tf_op jit(solution)/shard_map/concatenate | solution.py:72
  173.2 6.9 %copy.24 = f32[16384,61]{1,0:T(8,128)} copy(f32[16384,61]{0,1:T(8,128)} %bitcast.130) | data formatting | bytes 7995392 | tf_op jit(solution)/shard_map/concatenate | solution.py:72
  180.1 44.4 %scatter_custom_fusion = f32[61,16384]{0,1:T(8,128)} fusion(s32[16384]{0:T(1024)S(1)} %get-tuple-element.157, f32[16384,61]{1,0:T(8,128)} %copy.24, f32[]{:T(128)} %constant.86.clone.1), kind=kCustom, calls=%fused_computation.3 | custom fusion | bytes 3998208 | tf_op jit(solution)/shard_map/scatter | solution.py:84
  224.5 7.7 %gather_fusion = f32[128,61,128]{1,2,0:T(8,128)} fusion(f32[61,128,128]{0,2,1:T(8,128)} %bitcast.128, s32[1024]{0:T(1024)S(1)} %pad_clamp_fusion), kind=kCustom, calls=%fused_computation | custom fusion | bytes 7995904 | tf_op jit(solution)/shard_map/gather | solution.py:93
  232.2 1.8 fusion.15
  234.0 3.9 %reshape.632 = f32[8,1,31232]{2,1,0:T(1,128)} reshape(f32[8,16,32,61]{3,2,1,0:T(8,128)S(1)} %fusion.15) | data formatting | bytes 1998848
  237.9 5.5 %all-to-all-start.1 = ((f32[8,1,31232]{2,1,0:T(1,128)}), f32[8,1,31232]{2,1,0:T(1,128)S(1)}, u32[]{:S(2)}, u32[]{:S(2)}) async-start(f32[8,1,31232]{2,1,0:T(1,128)} %reshape.632), calls=%async_computation.1 | async-start | bytes 1998848 | tf_op jit(solution)/shard_map/all_to_all | solution.py:104
  244.8 22.6 %all-to-all-done.1 = f32[8,1,31232]{2,1,0:T(1,128)S(1)} async-done(((f32[8,1,31232]{2,1,0:T(1,128)}), f32[8,1,31232]{2,1,0:T(1,128)S(1)}, u32[]{:S(2)}, u32[]{:S(2)}) %all-to-all-start.1) | async-done | bytes 999456 | tf_op jit(solution)/shard_map/all_to_all | solution.py:104
  267.9 3.0 reduce.6
  270.9 4.3 %reshape.633 = f32[8,16,32,61]{3,2,1,0:T(8,128)} reshape(f32[8,31232]{1,0:T(8,128)S(1)} %reduce.6) | data formatting | bytes 1998848
  275.5 12.0 %scatter_fusion = f32[61,128,32]{0,2,1:T(8,128)S(1)} fusion(f32[61,128,32]{0,2,1:T(8,128)S(1)} %broadcast_in_dim.21, s32[128]{0:T(128)S(1)} %fusion.4, f32[128,61,32]{1,2,0:T(8,128)} %bitcast.129), kind=kCustom, calls=%fused_computation.2 | custom fusion | bytes 2998784 | tf_op jit(solution)/shard_map/scatter | solution.py:111
  289.4 19.8 %psum.7 = f32[]{:T(128)} all-reduce(f32[]{:T(128)S(6)} %convert_element_type.47), channel_id=1, replica_groups=mesh['view'=4,'gauss'=8] {'gauss'}, use_global_device_ids=true, to_apply=%region_10.11 | all-reduce | flops 1 | bytes 8 | tf_op jit(solution)/shard_map/psum | solution.py:79
  310.6 34.7 %all-gather.2.cloned.1.call-done = f32[61,128,128]{0,2,1:T(8,128)} async-done(((f32[61,128,32]{0,2,1:T(8,128)}), f32[61,128,128]{0,2,1:T(8,128)}) %all-gather.2.cloned.1.call-update) | async-done | bytes 3997712 | tf_op jit(solution)/shard_map/all_gather | solution.py:113
  345.3 6.8 %copy.25 = f32[61,16384]{1,0:T(8,128)} copy(f32[61,16384]{0,1:T(8,128)} %bitcast.131) | data formatting | bytes 7995392
  (69 shorter events, 24.1 us)
Async XLA Ops:
  7.2 66.7 %copy-start.1 = (f32[3,16384]{1,0:T(4,128)S(1)}, f32[3,16384]{1,0:T(4,128)}, u32[]{:S(2)}) copy-start(f32[3,16384]{1,0:T(4,128)} %param.12) | copy-start | bytes 589828
  7.2 107.9 %copy-start.7 = (s32[4,16384]{1,0:T(4,128)S(1)}, s32[4,16384]{1,0:T(4,128)}, u32[]{:S(2)}) copy-start(s32[4,16384]{1,0:T(4,128)} %param.17) | copy-start | bytes 786436
  8.2 107.1 %copy-start.3 = (f32[3,16384]{1,0:T(4,128)S(1)}, f32[3,16384]{1,0:T(4,128)}, u32[]{:S(2)}) copy-start(f32[3,16384]{1,0:T(4,128)} %param.13) | copy-start | bytes 589828
  8.8 106.7 %copy-start.4 = (f32[4,2,16384]{2,1,0:T(2,128)S(1)}, f32[4,2,16384]{2,1,0:T(2,128)}, u32[]{:S(2)}) copy-start(f32[4,2,16384]{2,1,0:T(2,128)} %param.16) | copy-start | bytes 1572868
  35.8 202.1 %all-to-all-start = ((s32[1,8,16]{2,0,1:T(1,128)}), s32[1,8,16]{2,0,1:T(1,128)S(1)}, u32[]{:S(2)}, u32[]{:S(2)}) async-start(s32[1,8,16]{2,0,1:T(1,128)} %compare_select_fusion.1), calls=%async_computation | async-start | bytes 8192 | tf_op jit(solution)/shard_map/all_to_all | solution.py:105
  39.1 112.5 %all-reduce.4.cloned.1.call-start = ((), (), s32[]{:S(2)}) async-start(), calls=%async_computation.3 | async-start | bytes 262144 | tf_op jit(solution)/shard_map/pmax | solution.py:70
  79.9 71.7 %copy-start.2 = (f32[4,16384]{1,0:T(4,128)S(1)}, f32[4,16384]{1,0:T(4,128)}, u32[]{:S(2)}) copy-start(f32[4,16384]{1,0:T(4,128)} %param.14) | copy-start | bytes 786436
  237.9 29.4 %all-to-all-start.1 = ((f32[8,1,31232]{2,1,0:T(1,128)}), f32[8,1,31232]{2,1,0:T(1,128)S(1)}, u32[]{:S(2)}, u32[]{:S(2)}) async-start(f32[8,1,31232]{2,1,0:T(1,128)} %reshape.632), calls=%async_computation.1 | async-start | bytes 1998848 | tf_op jit(solution)/shard_map/all_to_all | solution.py:104
  243.5 101.8 %all-gather.2.cloned.1.call-start = ((), (), s32[]{:S(2)}) async-start(), calls=%async_computation.2 | async-start | bytes 10485760 | tf_op jit(solution)/shard_map/all_gather | solution.py:113
  275.4 34.4 %copy-start.5 = (f32[1,16384]{1,0:T(1,128)S(1)}, f32[1,16384]{1,0:T(1,128)}, u32[]{:S(2)}) copy-start(f32[1,16384]{1,0:T(1,128)} %get-tuple-element.100) | copy-start | bytes 196612
  275.4 34.4 %copy-start.6 = (f32[1,16384]{1,0:T(1,128)S(1)}, f32[1,16384]{1,0:T(1,128)}, u32[]{:S(2)}) copy-start(f32[1,16384]{1,0:T(1,128)} %get-tuple-element.101) | copy-start | bytes 196612
  287.4 1.3 copy-start
Sparse Core Ops, SparseCore 0:
  118.4 33.1 all-reduce.3
  288.9 56.3 all-gather.1
where the time goes:
time: 363 us; the launch traced here: 360 us
  local copies, waits for them, and re-layouts  127 us (35%)
  waiting for transfers between devices  90.4 us (25%)
  other arithmetic  76.7 us (21%)
  blocking collectives  32.9 us (9%)
  between operations  19.9 us (5%)
  starting transfers between devices  8.9 us (2%)
  loops' own time  4.58 us (1%)
    add x8, other arithmetic, view_stats(): first = [j00 * rot[0, j] + j02 * rot[2, j] for j in range(3)]  53 us
    scatter x1, local copies, waits for them, and re-layouts, body(): jnp.zeros((feat_rows, cap_blk * 128), jnp.float32).at[:, where_to]  44.4 us
    all_gather x1, waiting for transfers between devices, body(): placed = lax.all_gather(partial_place, 'view', axis=2, tiled=True)  34.7 us
    pmax x1, waiting for transfers between devices, body(): gmax, rmax = lax.pmax((gmax, rmax), 'view')  33.1 us
    concatenate x2, local copies, waits for them, and re-layouts, body(): rows = jnp.concatenate([means, scales, quats, attrs, peak], axis=0)  28.5 us
    all_to_all x1, waiting for transfers between devices, body(): lax.all_to_all(portion, 'gauss', split_axis=1, concat_axis=1, tiled=True)  22.6 us
    psum x1, blocking collectives, body(): summed = lax.psum(count.astype(jnp.float32), 'gauss')  19.8 us
    unnamed x24, local copies, waits for them, and re-layouts  18.4 us
  transfers between devices with their start and end apart: 4, of which 3 were waited for; matrix products, arithmetic and copies ran while one was open for 46% of the time, Pallas kernels for 0%

commit v1 on v0

v1 whole, which is shorter than its diff:
```python
import functools

import jax
import jax.numpy as jnp
from jax import lax
from jax.experimental import pallas as pl
from jax.experimental.pallas import tpu as pltpu
from jax.sharding import PartitionSpec as P

LANES = 128
SUB = 8
ATTR_TILES = 6
TILES = ATTR_TILES + 2
VMEM = pltpu.VMEM
SMEM = pltpu.SMEM
MESH = pl.DeviceIdType.MESH


def spec(space):
    return pl.BlockSpec(memory_space=space)


def peer(view, gauss):
    return {"view": view, "gauss": gauss}


def quat_factor(scales, quats):
    w, x, y, z = quats
    inv = 1.0 / jnp.sqrt(w * w + x * x + y * y + z * z + 0.25)
    w, x, y, z = (w * inv, x * inv, y * inv, z * inv)
    rq = [
        [1 - 2 * (y * y + z * z), 2 * (x * y - w * z), 2 * (x * z + w * y)],
        [2 * (x * y + w * z), 1 - 2 * (x * x + z * z), 2 * (y * z - w * x)],
        [2 * (x * z - w * y), 2 * (y * z + w * x), 1 - 2 * (x * x + y * y)],
    ]
    return [[rq[i][j] * scales[j] for j in range(3)] for i in range(3)]


def view_radius(means, factor, rot, trans, focal_v):
    point = [
        rot[i][0] * means[0] + rot[i][1] * means[1] + rot[i][2] * means[2] + trans[i]
        for i in range(3)
    ]
    inv = 1.0 / jnp.maximum(point[2], 1.0)
    j00 = focal_v * inv
    j02 = -(j00 * point[0]) * inv
    j12 = -(j00 * point[1]) * inv
    first = [j00 * rot[0][j] + j02 * rot[2][j] for j in range(3)]
    second = [j00 * rot[1][j] + j12 * rot[2][j] for j in range(3)]
    prow = [sum((first[j] * factor[j][k] for j in range(3))) for k in range(3)]
    qrow = [sum((second[j] * factor[j][k] for j in range(3))) for k in range(3)]
    a_val = prow[0] * prow[0] + prow[1] * prow[1] + prow[2] * prow[2] + 0.3
    c_val = qrow[0] * qrow[0] + qrow[1] * qrow[1] + qrow[2] * qrow[2] + 0.3
    b_val = prow[0] * qrow[0] + prow[1] * qrow[1] + prow[2] * qrow[2]
    half = 0.5 * (a_val - c_val)
    lam = 0.5 * (a_val + c_val) + jnp.sqrt(half * half + b_val * b_val + 0.01)
    return 3.0 * jnp.sqrt(lam)


def stats_kernel(
    V, S, views, par, mask, means, scales, quats, grad, vis, peak, meta,
    cnt, counts, local, halves, merged, whole,
    csend, crecv, rsend, rrecv, gsend, grecv,
):
    v, s = lax.axis_index("view"), lax.axis_index("gauss")
    nblk = mask.shape[0]
    piece = 2 * nblk // V
    cnt[...] = jnp.full((SUB, LANES), jnp.sum(mask[...]), jnp.int32)
    bar = pltpu.get_barrier_semaphore()
    for k in range(1, S):
        pl.semaphore_signal(bar, inc=1, device_id=peer(v, lax.rem(s + k, S)), device_id_type=MESH)
    for k in range(1, V):
        pl.semaphore_signal(bar, inc=1, device_id=peer(lax.rem(v + k, V), s), device_id_type=MESH)

    step = 2 * SUB

    def chunk(i, carry):
        rows = pl.ds(pl.multiple_of(i * step, step), step)
        m = [means[c, rows, :] for c in range(3)]
        factor = quat_factor(
            [scales[c, rows, :] for c in range(3)], [quats[c, rows, :] for c in range(4)]
        )
        gmax = jnp.zeros((step, LANES), jnp.float32)
        rmax = jnp.zeros((step, LANES), jnp.float32)
        for u in range(views):
            rot = [[par[u * 13 + 3 * a + b] for b in range(3)] for a in range(3)]
            trans = [par[u * 13 + 9 + a] for a in range(3)]
            radius = view_radius(m, factor, rot, trans, par[u * 13 + 12])
            seen = vis[u, rows, :].astype(jnp.float32)
            g0, g1 = grad[u, 0, rows, :], grad[u, 1, rows, :]
            gmax = jnp.maximum(gmax, jnp.sqrt(g0 * g0 + g1 * g1) * seen)
            rmax = jnp.maximum(rmax, radius * seen)
        local[rows, :] = gmax
        local[pl.ds(pl.multiple_of(nblk + i * step, step), step), :] = rmax
        return carry

    lax.fori_loop(0, nblk // step, chunk, 0)
    pl.semaphore_wait(bar, S + V - 2)
    copies = []
    for k in range(1, V):
        to = lax.rem(v + k, V)
        rs = pltpu.make_async_remote_copy(
            src_ref=local.at[pl.ds(pl.multiple_of(to * piece, piece), piece), :],
            dst_ref=halves.at[k],
            send_sem=rsend.at[k],
            recv_sem=rrecv.at[k],
            device_id=peer(to, s),
            device_id_type=MESH,
        )
        rs.start()
        copies.append(rs)
    tally = []
    for k in range(1, S):
        cp = pltpu.make_async_remote_copy(
            src_ref=cnt,
            dst_ref=counts.at[k],
            send_sem=csend.at[k],
            recv_sem=crecv.at[k],
            device_id=peer(v, lax.rem(s + k, S)),
            device_id_type=MESH,
        )
        cp.start()
        tally.append(cp)
    for rs in copies:
        rs.wait_recv()
    mine = pl.ds(pl.multiple_of(v * piece, piece), piece)
    best = local[mine, :]
    for k in range(1, V):
        best = jnp.maximum(best, halves[k])
    merged[...] = best
    spread = []
    for k in range(1, V):
        ag = pltpu.make_async_remote_copy(
            src_ref=merged,
            dst_ref=whole.at[k],
            send_sem=gsend.at[k],
            recv_sem=grecv.at[k],
            device_id=peer(lax.rem(v + k, V), s),
            device_id_type=MESH,
        )
        ag.start()
        spread.append(ag)
    for cp in tally:
        cp.wait_recv()
    lane = lax.broadcasted_iota(jnp.int32, (SUB, LANES), 1)
    sub = lax.broadcasted_iota(jnp.int32, (SUB, LANES), 0)
    blocks = jnp.zeros((SUB, LANES), jnp.int32)
    offs = jnp.zeros((SUB, LANES), jnp.int32)
    total = jnp.zeros((SUB, LANES), jnp.int32)
    for k in range(S):
        c = cnt[...] if k == 0 else counts[k]
        who = lax.rem(s + S - k, S)
        b = (c + (LANES - 1)) // LANES
        blocks = jnp.where(lane == who, b, blocks)
        offs = offs + jnp.where(lane > who, b, 0)
        total = total + c
    meta[...] = jnp.where(sub == 0, blocks, jnp.where(sub == 1, offs, total))
    peak[mine, :] = best
    for k in range(1, V):
        spread[k - 1].wait_recv()
        who = lax.rem(v + V - k, V)
        peak[pl.ds(pl.multiple_of(who * piece, piece), piece), :] = whole[k]
    for cp in copies + tally + spread:
        cp.wait_send()


def pack_kernel(
    V, S, T, per, meta, mask, attrs, last, means, scales, quats, peak, out,
    x, enc, basev, bases, sem, sem2,
):
    v, s = lax.axis_index("view"), lax.axis_index("gauss")
    nblk = mask.shape[0]
    for j in range(T):
        tile = v * T + j

        @pl.when(tile < ATTR_TILES)
        def _():
            pltpu.make_async_copy(
                attrs.at[pl.ds(pl.multiple_of(tile * SUB, SUB), SUB), :], x.at[j], sem.at[j]
            ).start()

    m = mask[...]
    lane = lax.broadcasted_iota(jnp.int32, (nblk, LANES), 1)
    mb = m.astype(jnp.bfloat16)
    li = lax.broadcasted_iota(jnp.int32, (LANES, LANES), 0)
    lj = lax.broadcasted_iota(jnp.int32, (LANES, LANES), 1)
    before = (li < lj).astype(jnp.bfloat16)
    bi = lax.broadcasted_iota(jnp.int32, (nblk, nblk), 0)
    bj = lax.broadcasted_iota(jnp.int32, (nblk, nblk), 1)
    above = (bi > bj).astype(jnp.bfloat16)
    under = (bi < bj).astype(jnp.bfloat16)
    dot = functools.partial(jnp.dot, preferred_element_type=jnp.float32)
    ones = jnp.ones((LANES, LANES), jnp.bfloat16)
    rank = dot(mb, before).astype(jnp.int32)
    size = dot(mb, ones).astype(jnp.int32)
    base = dot(dot(above, mb).astype(jnp.bfloat16), ones).astype(jnp.int32)
    flat = lax.dot_general(
        jnp.ones((SUB, LANES), jnp.bfloat16), mb, (((1,), (1,)), ((), ())),
        preferred_element_type=jnp.float32,
    )
    starts = dot(flat.astype(jnp.bfloat16), under)
    top = lax.broadcasted_iota(jnp.int32, (SUB, nblk), 0) == 0
    basev[...] = jnp.where(top, starts, starts + flat).astype(jnp.int32)
    scal = pltpu.make_async_copy(basev, bases, sem2)
    scal.start()
    code = jnp.where(m == 1, 65536 + (lane - rank) * 256 + lane, 0)
    bit = 1
    while bit < LANES:
        moved = pltpu.roll(code, LANES - bit, 1)
        goes = (moved & (bit * 256)) != 0
        stays = (code & (bit * 256)) == 0
        code = jnp.where(goes, moved, jnp.where(stays, code, 0))
        bit *= 2
    turn = (lane - base) & (LANES - 1)
    src = jnp.take_along_axis(code & (LANES - 1), turn, axis=1)
    enc[...] = jnp.where(turn < size, src, -1)

    for j in range(T):
        tile = v * T + j

        @pl.when(tile == ATTR_TILES)
        def _():
            x[j, 0:3, :] = means[...]
            x[j, 3:6, :] = scales[...]
            x[j, 6:8, :] = quats[0:2, :]

        @pl.when(tile == ATTR_TILES + 1)
        def _():
            x[j, 0:2, :] = quats[2:4, :]
            x[j, 2:3, :] = last[...]
            x[j, 3:5, :] = peak[...]
            x[j, 5:8, :] = jnp.zeros((3, peak.shape[1]), jnp.float32)

        @pl.when(tile < ATTR_TILES)
        def _():
            pltpu.make_async_copy(attrs.at[pl.ds(0, SUB), :], x.at[j], sem.at[j]).wait()

    out[...] = jnp.zeros_like(out)
    scal.wait()
    offset = meta[1, s]
    row = lax.broadcasted_iota(jnp.int32, (SUB, LANES), 1)

    def spot(d):
        return jnp.where(d < nblk, lax.rem(offset + d, S) * per + lax.div(d, S), S * per)

    def move(b, cur):
        start = bases[0, b]
        off = lax.rem(start, LANES)
        d = lax.div(start, LANES)
        e = jnp.broadcast_to(enc[pl.ds(b, 1), :], (SUB, LANES))
        idx = jnp.maximum(e, 0)
        ok = e >= 0
        low = ok & (row >= off)
        high = ok & (row < off)
        where = spot(d)
        cols = pl.ds(pl.multiple_of(b * LANES, LANES), LANES)
        full = bases[1, b] >= (d + 1) * LANES
        nxt = []
        for j in range(T):
            g = jnp.take_along_axis(x[j, :, cols], idx, axis=1)
            keep = jnp.where(low, g, cur[j])
            out[where, j * SUB:(j + 1) * SUB, :] = keep
            nxt.append(jnp.where(full, jnp.where(high, g, 0.0), keep))
        return tuple(nxt)

    zero = jnp.zeros((SUB, LANES), jnp.float32)
    cur = lax.fori_loop(0, nblk, move, (zero,) * T)
    end = lax.div(bases[1, nblk - 1], LANES)
    for j in range(T):
        out[spot(end), j * SUB:(j + 1) * SUB, :] = cur[j]


def ship_kernel(V, S, per, src, buf, gsend, vsend, csend, recv, lsem):
    v, s = lax.axis_index("view"), lax.axis_index("gauss")
    core = lax.rem(v, 2)
    mate = v + 1 - 2 * core
    X = V // 2
    bar = pltpu.get_barrier_semaphore()
    for k in range(1, S):
        pl.semaphore_signal(bar, inc=1, device_id=peer(v, lax.rem(s + k, S)), device_id_type=MESH)
    for q in range(1, X):
        pl.semaphore_signal(
            bar, inc=1, device_id=peer(lax.rem(v + 2 * q, V), s), device_id_type=MESH
        )
    pl.semaphore_signal(bar, inc=1, device_id=peer(mate, s), device_id_type=MESH)
    pl.semaphore_wait(bar, S - 1 + X)

    def part(i):
        return pl.ds(i * per, per)

    def far(k):
        to = lax.rem(s + k, S)
        return pltpu.make_async_remote_copy(
            src_ref=src.at[part(to)], dst_ref=buf.at[v, part(s)],
            send_sem=gsend.at[k], recv_sem=recv.at[0, k],
            device_id=peer(v, to), device_id_type=MESH,
        )

    def at(k, q):
        owner = lax.rem(v + V - 2 * q, V)
        frm = lax.rem(s + S - k, S)
        if k == 0 and q == 0:
            return src.at[part(s)], owner, frm
        return buf.at[owner, part(frm)], owner, frm

    def across(k, q):
        ref, _, frm = at(k, 0)
        return pltpu.make_async_remote_copy(
            src_ref=ref, dst_ref=buf.at[v, part(frm)],
            send_sem=vsend.at[q, k], recv_sem=recv.at[q, k],
            device_id=peer(lax.rem(v + 2 * q, V), s), device_id_type=MESH,
        )

    def beside(k, q):
        ref, owner, frm = at(k, q)
        return pltpu.make_async_remote_copy(
            src_ref=ref, dst_ref=buf.at[owner, part(frm)],
            send_sem=csend.at[q, k], recv_sem=recv.at[X + q, k],
            device_id=peer(mate, s), device_id_type=MESH,
        )

    started = []

    def go(copy):
        copy.start()
        started.append(copy)

    fars = {k: far(k) for k in range(1, S)}
    for k in range(1, S):
        go(fars[k])
    for q in range(1, X):
        go(across(0, q))
    go(beside(0, 0))
    own = pltpu.make_async_copy(src.at[part(s)], buf.at[v, part(s)], lsem)
    own.start()
    for k in range(S):
        if k:
            fars[k].wait_recv()
            for q in range(1, X):
                go(across(k, q))
            go(beside(k, 0))
        if k:
            for q in range(1, X):
                across(k - 1, q).wait_recv()
                go(beside(k - 1, q))
    for q in range(1, X):
        across(S - 1, q).wait_recv()
        go(beside(S - 1, q))
    for k in range(S):
        for q in range(X):
            beside(k, q).wait_recv()
    for copy in started:
        copy.wait_send()
    own.wait()


def place_kernel(S, T, per, meta, buf, out):
    me = lax.axis_index("gauss")
    slots = out.shape[1] // LANES
    sub = lax.broadcasted_iota(jnp.int32, (SUB, LANES), 0)
    rows = out.shape[0]
    head = sub < 2
    filled = jnp.int32(0)
    for s in range(S):
        blocks, offset = meta[0, s], meta[1, s]
        first = lax.rem(me + S - lax.rem(offset, S), S)
        n = lax.div(jnp.maximum(blocks - first, 0) + (S - 1), S)
        slot0 = lax.div(offset + first, S)

        def one(w, carry):
            t = []
            for tile in range(TILES):
                j = tile % T
                t.append(buf[tile // T, s * per + w, j * SUB:(j + 1) * SUB, :])
            turned = [pltpu.roll(a, 2, 0) for a in t[:ATTR_TILES]]
            mixed = t[ATTR_TILES + 1]
            chain = [mixed] + turned + [mixed]
            cols = pl.ds(pl.multiple_of((slot0 + w) * LANES, LANES), LANES)
            out[0:SUB, cols] = t[ATTR_TILES]
            for i in range(1, TILES):
                value = jnp.where(head, chain[i - 1], chain[i])
                hi = min((i + 1) * SUB, rows)
                out[i * SUB:hi, cols] = value[: hi - i * SUB]
            return carry

        lax.fori_loop(0, n, one, 0)
        filled = filled + n

    def clear(q, carry):
        cols = pl.ds(pl.multiple_of(q * LANES, LANES), LANES)
        out[:, cols] = jnp.zeros((rows, LANES), jnp.float32)
        return carry

    lax.fori_loop(filled, slots, clear, 0)


def body(V, S, means, scales, quats, attrs, grad_screen, visible, clone_mask, rotation, shift, focal):
    G = clone_mask.shape[0]
    nblk = G // LANES
    views = grad_screen.shape[0]
    rows = means.shape[0] + scales.shape[0] + quats.shape[0] + attrs.shape[0] + 2
    T = -(-TILES // V)
    per = -(-nblk // S)
    f32, i32 = jnp.float32, jnp.int32
    mask = clone_mask.reshape(nblk, LANES)
    par = jnp.concatenate(
        [rotation.reshape(views, 9), shift, focal[:, None]], axis=1
    ).reshape(-1)
    dma = pltpu.SemaphoreType.DMA
    piece = 2 * nblk // V
    peak2, meta = pl.pallas_call(
        functools.partial(stats_kernel, V, S, views),
        out_shape=(
            jax.ShapeDtypeStruct((2 * nblk, LANES), f32),
            jax.ShapeDtypeStruct((SUB, LANES), i32),
        ),
        in_specs=[spec(SMEM)] + [spec(VMEM)] * 6,
        out_specs=(spec(VMEM), spec(VMEM)),
        scratch_shapes=[
            VMEM((SUB, LANES), i32),
            VMEM((S, SUB, LANES), i32),
            VMEM((2 * nblk, LANES), f32),
            VMEM((V, piece, LANES), f32),
            VMEM((piece, LANES), f32),
            VMEM((V, piece, LANES), f32),
            dma((S,)), dma((S,)), dma((V,)), dma((V,)), dma((V,)), dma((V,)),
        ],
        compiler_params=pltpu.CompilerParams(collective_id=0, has_side_effects=True),
        name="stats",
    )(
        par, mask,
        means.reshape(3, nblk, LANES), scales.reshape(3, nblk, LANES),
        quats.reshape(4, nblk, LANES), grad_screen.reshape(views, 2, nblk, LANES),
        visible.reshape(views, nblk, LANES),
    )
    peak = peak2.reshape(2, G)
    total = meta[2, 0]
    R = T * SUB
    packed = pl.pallas_call(
        functools.partial(pack_kernel, V, S, T, per),
        out_shape=jax.ShapeDtypeStruct((S * per + 1, R, LANES), f32),
        in_specs=[spec(SMEM), spec(VMEM), spec(pl.ANY)] + [spec(VMEM)] * 5,
        out_specs=spec(VMEM),
        scratch_shapes=[
            VMEM((T, SUB, G), f32),
            VMEM((nblk, LANES), i32),
            VMEM((SUB, nblk), i32),
            SMEM((SUB, nblk), i32),
            dma((T,)), dma,
        ],
        name="pack",
    )(meta, mask, attrs, attrs[ATTR_TILES * SUB:], means, scales, quats, peak)
    X = V // 2
    buf = pl.pallas_call(
        functools.partial(ship_kernel, V, S, per),
        out_shape=jax.ShapeDtypeStruct((V, S * per, R, LANES), f32),
        in_specs=[spec(VMEM)],
        out_specs=spec(pl.ANY),
        scratch_shapes=[
            dma((S,)), dma((X, S)), dma((X, S)), dma((2 * X, S)), dma,
        ],
        compiler_params=pltpu.CompilerParams(collective_id=1, has_side_effects=True),
        name="ship",
    )(packed)
    clones = pl.pallas_call(
        functools.partial(place_kernel, S, T, per),
        out_shape=jax.ShapeDtypeStruct((rows, G), f32),
        in_specs=[spec(SMEM), spec(VMEM)],
        out_specs=spec(VMEM),
        compiler_params=pltpu.CompilerParams(vmem_limit_bytes=32 * 1024 * 1024),
        name="place",
    )(meta, buf)
    return peak, clones, total


def solution(mesh):
    return jax.shard_map(
        functools.partial(body, mesh.shape["view"], mesh.shape["gauss"]),
        mesh=mesh,
        in_specs=(
            P(None, "gauss"),
            P(None, "gauss"),
            P(None, "gauss"),
            P(None, "gauss"),
            P("view", None, "gauss"),
            P("view", "gauss"),
            P("gauss"),
            P("view", None, None),
            P("view", None),
            P("view"),
        ),
        out_specs=(P(None, "gauss"), P(None, "gauss"), P()),
        check_vma=False,
    )
```

time: 363 us -> 90.4 us (0.25)
  the two profiles are of different devices: /device:TPU:0 before, /device:TPU:25 now
where the time goes in v1:
time: 90.4 us; the launch traced here: 89.9 us
  Pallas kernels  72.9 us (81%)
  local copies, waits for them, and re-layouts  15.5 us (17%)
    pallas_call x1, Pallas kernels, body(): pl.pallas_call(functools.partial(ship_kernel, V, S, per), out_shape=jax.S...  44.8 us
    pallas_call x1, Pallas kernels, body(): pl.pallas_call(functools.partial(pack_kernel, V, S, T, per), out_shape=ja...  13.8 us
    pallas_call x1, Pallas kernels, body(): pl.pallas_call(functools.partial(stats_kernel, V, S, views), out_shape=(j...  10.8 us
    unnamed x7, local copies, waits for them, and re-layouts  6.19 us
    pallas_call x1, Pallas kernels, body(): pl.pallas_call(functools.partial(place_kernel, S, T, per), out_shape=jax....  3.47 us
    reshape x1, local copies, waits for them, and re-layouts, body(): grad_screen.reshape(views, 2, nblk, LANES)  2.28 us

profile of v1, /device:TPU:25, one launch (start us, length us, event | category | flops | bytes accessed | tf_op | source)
XLA Modules:
  0.0 89.9 jit_solution(17466201376527818857)
XLA Ops:
  0.6 1.8 %copy_bitcast_fusion.2 = (f32[3,128,128]{2,1,0:T(8,128)}, f32[3,128,128]{2,1,0:T(8,128)}) fusion(f32[1,3,128,128]{3,1,2,0:T(4,128)} %bitcast.17, f32[1,3,128,128]{3,1,2,0:T(4,128)} %bitcast.18), kind=kLoop, calls=%fused_computation.2 | loop fusion | bytes 786432 | tf_op jit(solution)/shard_map/reshape | solution.py:432
  2.4 2.3 %reshape.39.grad = f32[4,2,128,128]{3,2,1,0:T(8,128)} reshape(f32[4,2,16384]{2,1,0:T(2,128)} %param.14) | data formatting | bytes 1048576 | tf_op jit(solution)/shard_map/reshape | solution.py:433
  4.7 1.7 %copy.25 = s32[1,4,128,128]{3,2,1,0:T(8,128)} copy(s32[1,4,128,128]{3,1,2,0:T(4,128)} %bitcast.24) | data formatting | bytes 524288
  6.4 1.7 %copy.26 = f32[1,4,128,128]{3,2,1,0:T(8,128)} copy(f32[1,4,128,128]{3,1,2,0:T(4,128)} %bitcast.19) | data formatting | bytes 524288
  8.0 0.7 copy.15
  8.7 0.1 reshape.33
  8.8 0.7 copy.16
  9.6 0.8 pad_maximum_fusion
  10.3 0.6 reshape.34.par
  10.9 10.8 %stats.1 = (f32[256,128]{1,0:T(8,128)}, s32[8,128]{1,0:T(8,128)}) custom-call(f32[52]{0:T(128)} %reshape.34.par, s32[128,128]{1,0:T(8,128)} %bitcast.22, f32[3,128,128]{2,1,0:T(8,128)} %get-tuple-element.8.means, f32[3,128,128]{2,1,0:T(8,128)} %get-tuple-element.7.scales, f32[4,128,128]{2,1,0:T(8,128)} %bitcast.21, f32[4,2,128,128]{3,2,1,0:T(8,128)} %reshape.39.grad, ...), custom_call_target="tpu_custom_call" | custom-call | tf_op jit(solution)/shard_map/stats/pallas_call | solution.py:411
  21.7 1.6 %reshape.41.peak = f32[2,16384]{1,0:T(2,128)} reshape(f32[256,128]{1,0:T(8,128)} %get-tuple-element.5) | data formatting | bytes 262144 | tf_op jit(solution)/shard_map/reshape | solution.py:436
  23.4 1.7 %slice.6.last = f32[1,16384]{1,0:T(1,128)} slice(f32[49,16384]{1,0:T(8,128)} %attrs.1), slice={[48:49], [0:16384]} | slice | bytes 131072 | tf_op jit(solution)/shard_map/slice | solution.py:452
  25.1 0.0 copy-start.1
  25.1 13.8 %pack.1.src = f32[129,16,128]{2,1,0:T(8,128)} custom-call(s32[8,128]{1,0:T(8,128)} %get-tuple-element.6.meta, s32[128,128]{1,0:T(8,128)} %bitcast.23, f32[49,16384]{1,0:T(8,128)} %attrs.1, f32[1,16384]{1,0:T(1,128)} %slice.6.last, f32[3,16384]{1,0:T(4,128)} %means.1, f32[3,16384]{1,0:T(4,128)} %scales.1, f32[4,16384]{1,0:T(4,128)} %quats.1, ...), custom_call_target="tpu_custom_call" | custom-call | tf_op jit(solution)/shard_map/pack/pallas_call | solution.py:439
  38.9 44.8 %ship.1.buf = f32[4,128,16,128]{3,2,1,0:T(8,128)} custom-call(f32[129,16,128]{2,1,0:T(8,128)} %pack.1.src), custom_call_target="tpu_custom_call" | custom-call | tf_op jit(solution)/shard_map/ship/pallas_call | solution.py:454
  83.7 0.0 copy-done.1
  83.7 0.0 copy-start
  83.7 2.2 %copy-done = f32[4,128,16,128]{3,2,1,0:T(8,128)S(1)} copy-done((f32[4,128,16,128]{3,2,1,0:T(8,128)S(1)}, f32[4,128,16,128]{3,2,1,0:T(8,128)}, u32[]{:S(2)}) %copy-start) | copy-done | bytes 4194328
  85.9 3.5 %place.1 = f32[61,16384]{1,0:T(8,128)} custom-call(s32[8,128]{1,0:T(8,128)S(1)} %copy-done.1, f32[4,128,16,128]{3,2,1,0:T(8,128)S(1)} %copy-done), custom_call_target="tpu_custom_call" | custom-call | tf_op jit(solution)/shard_map/place/pallas_call | solution.py:465
  89.4 0.5 slice.7
Async XLA Ops:
  25.1 58.7 %copy-start.1 = (s32[8,128]{1,0:T(8,128)S(1)}, s32[8,128]{1,0:T(8,128)}, u32[]{:S(2)}) copy-start(s32[8,128]{1,0:T(8,128)} %get-tuple-element.6.meta) | copy-start | bytes 12292
  83.7 2.2 %copy-start = (f32[4,128,16,128]{3,2,1,0:T(8,128)S(1)}, f32[4,128,16,128]{3,2,1,0:T(8,128)}, u32[]{:S(2)}) copy-start(f32[4,128,16,128]{3,2,1,0:T(8,128)} %ship.1.buf) | copy-start | bytes 12582916

commit v2 on v1

--- a/solution.py
+++ b/solution.py
@@ -58,8 +58,8 @@
 
 
 def stats_kernel(
-    V, S, views, par, mask, means, scales, quats, grad, vis, peak, meta,
-    cnt, counts, local, halves, merged, whole,
+    V, S, views, rots, trns, foc, mask, means, scales, quats, grad, vis, peak, meta,
+    cnt, counts, local, halves, merged, whole, total_max,
     csend, crecv, rsend, rrecv, gsend, grecv,
 ):
     v, s = lax.axis_index("view"), lax.axis_index("gauss")
@@ -76,22 +76,26 @@
 
     def chunk(i, carry):
         rows = pl.ds(pl.multiple_of(i * step, step), step)
-        m = [means[c, rows, :] for c in range(3)]
+
+        def lines(ref, count, c):
+            return ref[pl.ds(i * step * count + c, step, stride=count), :]
+
+        m = [means[rows, c, :] for c in range(3)]
         factor = quat_factor(
-            [scales[c, rows, :] for c in range(3)], [quats[c, rows, :] for c in range(4)]
+            [scales[rows, c, :] for c in range(3)], [lines(quats, 4, c) for c in range(4)]
         )
         gmax = jnp.zeros((step, LANES), jnp.float32)
         rmax = jnp.zeros((step, LANES), jnp.float32)
         for u in range(views):
-            rot = [[par[u * 13 + 3 * a + b] for b in range(3)] for a in range(3)]
-            trans = [par[u * 13 + 9 + a] for a in range(3)]
-            radius = view_radius(m, factor, rot, trans, par[u * 13 + 12])
-            seen = vis[u, rows, :].astype(jnp.float32)
-            g0, g1 = grad[u, 0, rows, :], grad[u, 1, rows, :]
+            rot = [[rots[u, a, b] for b in range(3)] for a in range(3)]
+            trans = [trns[u, a] for a in range(3)]
+            radius = view_radius(m, factor, rot, trans, foc[u])
+            seen = lines(vis, views, u).astype(jnp.float32)
+            g0, g1 = (grad[u, pl.ds(i * step * 2 + c, step, stride=2), :] for c in range(2))
             gmax = jnp.maximum(gmax, jnp.sqrt(g0 * g0 + g1 * g1) * seen)
             rmax = jnp.maximum(rmax, radius * seen)
-        local[rows, :] = gmax
-        local[pl.ds(pl.multiple_of(nblk + i * step, step), step), :] = rmax
+        local[pl.ds(i * step * 2, step, stride=2), :] = gmax
+        local[pl.ds(i * step * 2 + 1, step, stride=2), :] = rmax
         return carry
 
     lax.fori_loop(0, nblk // step, chunk, 0)
@@ -155,17 +159,19 @@
         offs = offs + jnp.where(lane > who, b, 0)
         total = total + c
     meta[...] = jnp.where(sub == 0, blocks, jnp.where(sub == 1, offs, total))
-    peak[mine, :] = best
+    total_max[mine, :] = best
     for k in range(1, V):
         spread[k - 1].wait_recv()
         who = lax.rem(v + V - k, V)
-        peak[pl.ds(pl.multiple_of(who * piece, piece), piece), :] = whole[k]
+        total_max[pl.ds(pl.multiple_of(who * piece, piece), piece), :] = whole[k]
+    for c in range(2):
+        peak[:, c, :] = total_max[pl.ds(c, nblk, stride=2), :]
     for cp in copies + tally + spread:
         cp.wait_send()
 
 
 def pack_kernel(
-    V, S, T, per, meta, mask, attrs, last, means, scales, quats, peak, out,
+    V, S, T, per, meta, mask, attrs, means, scales, quats, peak, out,
     x, enc, basev, bases, sem, sem2,
 ):
     v, s = lax.axis_index("view"), lax.axis_index("gauss")
@@ -177,6 +183,12 @@
         def _():
             pltpu.make_async_copy(
                 attrs.at[pl.ds(pl.multiple_of(tile * SUB, SUB), SUB), :], x.at[j], sem.at[j]
+            ).start()
+
+        @pl.when(tile == ATTR_TILES + 1)
+        def _():
+            pltpu.make_async_copy(
+                attrs.at[pl.ds(ATTR_TILES * SUB, 1), :], x.at[j, pl.ds(2, 1), :], sem.at[j]
             ).start()
 
     m = mask[...]
@@ -227,9 +239,11 @@
         @pl.when(tile == ATTR_TILES + 1)
         def _():
             x[j, 0:2, :] = quats[2:4, :]
-            x[j, 2:3, :] = last[...]
             x[j, 3:5, :] = peak[...]
             x[j, 5:8, :] = jnp.zeros((3, peak.shape[1]), jnp.float32)
+            pltpu.make_async_copy(
+                attrs.at[pl.ds(ATTR_TILES * SUB, 1), :], x.at[j, pl.ds(2, 1), :], sem.at[j]
+            ).wait()
 
         @pl.when(tile < ATTR_TILES)
         def _():
@@ -264,7 +278,7 @@
         return tuple(nxt)
 
     zero = jnp.zeros((SUB, LANES), jnp.float32)
-    cur = lax.fori_loop(0, nblk, move, (zero,) * T)
+    cur = lax.fori_loop(0, nblk, move, (zero,) * T, unroll=8)
     end = lax.div(bases[1, nblk - 1], LANES)
     for j in range(T):
         out[spot(end), j * SUB:(j + 1) * SUB, :] = cur[j]
@@ -403,18 +417,20 @@
     per = -(-nblk // S)
     f32, i32 = jnp.float32, jnp.int32
     mask = clone_mask.reshape(nblk, LANES)
-    par = jnp.concatenate(
-        [rotation.reshape(views, 9), shift, focal[:, None]], axis=1
-    ).reshape(-1)
+
+    def lines(a):
+        a = a.reshape(a.shape[:-1] + (nblk, LANES))
+        return jnp.swapaxes(a, -3, -2)
+
     dma = pltpu.SemaphoreType.DMA
     piece = 2 * nblk // V
     peak2, meta = pl.pallas_call(
         functools.partial(stats_kernel, V, S, views),
         out_shape=(
-            jax.ShapeDtypeStruct((2 * nblk, LANES), f32),
+            jax.ShapeDtypeStruct((nblk, 2, LANES), f32),
             jax.ShapeDtypeStruct((SUB, LANES), i32),
         ),
-        in_specs=[spec(SMEM)] + [spec(VMEM)] * 6,
+        in_specs=[spec(SMEM)] * 3 + [spec(VMEM)] * 6,
         out_specs=(spec(VMEM), spec(VMEM)),
         scratch_shapes=[
             VMEM((SUB, LANES), i32),
@@ -423,23 +439,23 @@
             VMEM((V, piece, LANES), f32),
             VMEM((piece, LANES), f32),
             VMEM((V, piece, LANES), f32),
+            VMEM((2 * nblk, LANES), f32),
             dma((S,)), dma((S,)), dma((V,)), dma((V,)), dma((V,)), dma((V,)),
         ],
         compiler_params=pltpu.CompilerParams(collective_id=0, has_side_effects=True),
         name="stats",
     )(
-        par, mask,
-        means.reshape(3, nblk, LANES), scales.reshape(3, nblk, LANES),
-        quats.reshape(4, nblk, LANES), grad_screen.reshape(views, 2, nblk, LANES),
-        visible.reshape(views, nblk, LANES),
+        rotation, shift, focal, mask, lines(means), lines(scales),
+        lines(quats).reshape(-1, LANES), lines(grad_screen).reshape(views, -1, LANES),
+        lines(visible).reshape(-1, LANES),
     )
-    peak = peak2.reshape(2, G)
+    peak = jnp.swapaxes(peak2, 0, 1).reshape(2, G)
     total = meta[2, 0]
     R = T * SUB
     packed = pl.pallas_call(
         functools.partial(pack_kernel, V, S, T, per),
         out_shape=jax.ShapeDtypeStruct((S * per + 1, R, LANES), f32),
-        in_specs=[spec(SMEM), spec(VMEM), spec(pl.ANY)] + [spec(VMEM)] * 5,
+        in_specs=[spec(SMEM), spec(VMEM), spec(pl.ANY)] + [spec(VMEM)] * 4,
         out_specs=spec(VMEM),
         scratch_shapes=[
             VMEM((T, SUB, G), f32),
@@ -449,7 +465,7 @@
             dma((T,)), dma,
         ],
         name="pack",
-    )(meta, mask, attrs, attrs[ATTR_TILES * SUB:], means, scales, quats, peak)
+    )(meta, mask, attrs, means, scales, quats, peak)
     X = V // 2
     buf = pl.pallas_call(
         functools.partial(ship_kernel, V, S, per),

time: 90.4 us -> 73.2 us (0.81)
  local copies, waits for them, and re-layouts: 15.5 us -> 4.65 us
  Pallas kernels: 72.9 us -> 67.5 us
    pallas_call x1, Pallas kernels: 13.8 us -> 5.6 us  [body(): pl.pallas_call(functools.partial(pack_kernel, V, S, T, per), out_shape=ja...]
    reshape x5 -> x0, local copies, waits for them, and re-layouts: 6.41 us -> none  [the longest x1 2.28 us: body(): grad_screen.reshape(views, 2, nblk, LANES)]
    pallas_call x1, Pallas kernels: 10.8 us -> 14.4 us  [body(): pl.pallas_call(functools.partial(stats_kernel, V, S, views), out_shape=(j...]
    unnamed x7 -> x8, local copies, waits for them, and re-layouts: 6.19 us -> 4.14 us
    slice x1 -> x0, local copies, waits for them, and re-layouts: 1.69 us -> none  [body(): attrs[ATTR_TILES * SUB:]]
where the time goes in v2:
time: 73.2 us; the launch traced here: 72.9 us
  Pallas kernels  67.5 us (92%)
  local copies, waits for them, and re-layouts  4.65 us (6%)
    pallas_call x1, Pallas kernels, body(): pl.pallas_call(functools.partial(ship_kernel, V, S, per), out_shape=jax.S...  44.1 us
    pallas_call x1, Pallas kernels, body(): pl.pallas_call(functools.partial(stats_kernel, V, S, views), out_shape=(j...  14.4 us
    pallas_call x1, Pallas kernels, body(): pl.pallas_call(functools.partial(pack_kernel, V, S, T, per), out_shape=ja...  5.6 us
    unnamed x8, local copies, waits for them, and re-layouts  4.14 us
    pallas_call x1, Pallas kernels, body(): pl.pallas_call(functools.partial(place_kernel, S, T, per), out_shape=jax....  3.48 us

profile of v2, /device:TPU:25, one launch (start us, length us, event | category | flops | bytes accessed | tf_op | source)
XLA Modules:
  0.0 72.9 jit_solution(17762223885553974930)
XLA Ops:
  0.6 1.3 %copy.16.rots = f32[4,3,3]{2,1,0:T(4,128)} copy(f32[4,3,3]{2,0,1:T(4,128)} %param.17) | data formatting | bytes 288 | tf_op args[7]
  1.9 14.4 %stats.1 = (f32[128,2,128]{2,1,0:T(2,128)}, s32[8,128]{1,0:T(8,128)}) custom-call(f32[4,3,3]{2,1,0:T(4,128)} %copy.16.rots, f32[4,3]{1,0:T(4,128)} %trns.1, f32[4]{0:T(128)} %foc.1, s32[128,128]{1,0:T(8,128)} %bitcast.32, f32[128,3,128]{2,1,0:T(4,128)} %bitcast.26, f32[128,3,128]{2,1,0:T(4,128)} %bitcast.27, f32[512,128]{1,0:T(8,128)} %bitcast.28, ...), custom_call_target="tpu_custom_call" | custom-call | tf_op jit(solution)/shard_map/stats/pallas_call | solution.py:427
  16.3 0.0 copy-start.1
  16.3 5.6 %pack.1.src = f32[129,16,128]{2,1,0:T(8,128)} custom-call(s32[8,128]{1,0:T(8,128)} %get-tuple-element.6.meta, s32[128,128]{1,0:T(8,128)} %bitcast.33, f32[49,16384]{1,0:T(8,128)} %attrs.1, f32[3,16384]{1,0:T(4,128)} %means.1, f32[3,16384]{1,0:T(4,128)} %scales.1, f32[4,16384]{1,0:T(4,128)} %quats.1, f32[2,16384]{1,0:T(2,128)} %bitcast.30), custom_call_target="tpu_custom_call" | custom-call | tf_op jit(solution)/shard_map/pack/pallas_call | solution.py:455
  21.9 44.1 %ship.1.buf = f32[4,128,16,128]{3,2,1,0:T(8,128)} custom-call(f32[129,16,128]{2,1,0:T(8,128)} %pack.1.src), custom_call_target="tpu_custom_call" | custom-call | tf_op jit(solution)/shard_map/ship/pallas_call | solution.py:470
  66.0 0.0 copy-done.1
  66.0 0.0 copy-start
  66.0 2.2 %copy-done = f32[4,128,16,128]{3,2,1,0:T(8,128)S(1)} copy-done((f32[4,128,16,128]{3,2,1,0:T(8,128)S(1)}, f32[4,128,16,128]{3,2,1,0:T(8,128)}, u32[]{:S(2)}) %copy-start) | copy-done | bytes 4194328
  68.2 0.0 copy-start.2
  68.2 3.5 %place.1 = f32[61,16384]{1,0:T(8,128)} custom-call(s32[8,128]{1,0:T(8,128)S(1)} %copy-done.1, f32[4,128,16,128]{3,2,1,0:T(8,128)S(1)} %copy-done), custom_call_target="tpu_custom_call" | custom-call | tf_op jit(solution)/shard_map/place/pallas_call | solution.py:481
  71.7 0.5 slice.3
  72.2 0.0 copy-done.2
  72.2 0.7 copy.18
Async XLA Ops:
  16.3 49.7 %copy-start.1 = (s32[8,128]{1,0:T(8,128)S(1)}, s32[8,128]{1,0:T(8,128)}, u32[]{:S(2)}) copy-start(s32[8,128]{1,0:T(8,128)} %get-tuple-element.6.meta) | copy-start | bytes 12292
  66.0 2.2 %copy-start = (f32[4,128,16,128]{3,2,1,0:T(8,128)S(1)}, f32[4,128,16,128]{3,2,1,0:T(8,128)}, u32[]{:S(2)}) copy-start(f32[4,128,16,128]{3,2,1,0:T(8,128)} %ship.1.buf) | copy-start | bytes 12582916
  68.2 4.0 %copy-start.2 = (f32[128,2,128]{2,1,0:T(2,128)S(1)}, f32[128,2,128]{2,1,0:T(2,128)}, u32[]{:S(2)}) copy-start(f32[128,2,128]{2,1,0:T(2,128)} %get-tuple-element.5) | copy-start | bytes 393220

commit v3 on v2

--- a/solution.py
+++ b/solution.py
@@ -284,6 +284,17 @@
         out[spot(end), j * SUB:(j + 1) * SUB, :] = cur[j]
 
 
+def pair(s, k, S):
+    if S & (S - 1):
+        return lax.rem(s + k, S), lax.rem(s + S - k, S)
+    t, bit = s, 1
+    while bit < S:
+        if k & bit:
+            t = t + bit * (1 - 2 * lax.rem(lax.div(s, bit), 2))
+        bit *= 2
+    return t, t
+
+
 def ship_kernel(V, S, per, src, buf, gsend, vsend, csend, recv, lsem):
     v, s = lax.axis_index("view"), lax.axis_index("gauss")
     core = lax.rem(v, 2)
@@ -303,7 +314,7 @@
         return pl.ds(i * per, per)
 
     def far(k):
-        to = lax.rem(s + k, S)
+        to = pair(s, k, S)[0]
         return pltpu.make_async_remote_copy(
             src_ref=src.at[part(to)], dst_ref=buf.at[v, part(s)],
             send_sem=gsend.at[k], recv_sem=recv.at[0, k],
@@ -312,7 +323,7 @@
 
     def at(k, q):
         owner = lax.rem(v + V - 2 * q, V)
-        frm = lax.rem(s + S - k, S)
+        frm = pair(s, k, S)[1]
         if k == 0 and q == 0:
             return src.at[part(s)], owner, frm
         return buf.at[owner, part(frm)], owner, frm

time: 73.2 us -> 67.2 us (0.918)
  the two profiles are of different devices: /device:TPU:25 before, /device:TPU:0 now
where the time goes in v3:
time: 67.2 us; the launch traced here: 66.8 us
  Pallas kernels  61.5 us (92%)
  local copies, waits for them, and re-layouts  4.65 us (7%)
  between operations  0.68 us (1%)
    pallas_call x1, Pallas kernels, body(): pl.pallas_call(functools.partial(ship_kernel, V, S, per), out_shape=jax.S...  37 us
    pallas_call x1, Pallas kernels, body(): pl.pallas_call(functools.partial(stats_kernel, V, S, views), out_shape=(j...  15.4 us
    pallas_call x1, Pallas kernels, body(): pl.pallas_call(functools.partial(pack_kernel, V, S, T, per), out_shape=ja...  5.6 us
    unnamed x8, local copies, waits for them, and re-layouts  4.14 us
    pallas_call x1, Pallas kernels, body(): pl.pallas_call(functools.partial(place_kernel, S, T, per), out_shape=jax....  3.47 us

profile of v3, /device:TPU:0, one launch (start us, length us, event | category | flops | bytes accessed | tf_op | source)
XLA Modules:
  0.0 66.8 jit_solution(6344125951935896334)
XLA Ops:
  0.6 1.3 %copy.16.rots = f32[4,3,3]{2,1,0:T(4,128)} copy(f32[4,3,3]{2,0,1:T(4,128)} %param.17) | data formatting | bytes 288 | tf_op args[7]
  1.9 15.4 %stats.1 = (f32[128,2,128]{2,1,0:T(2,128)}, s32[8,128]{1,0:T(8,128)}) custom-call(f32[4,3,3]{2,1,0:T(4,128)} %copy.16.rots, f32[4,3]{1,0:T(4,128)} %trns.1, f32[4]{0:T(128)} %foc.1, s32[128,128]{1,0:T(8,128)} %bitcast.32, f32[128,3,128]{2,1,0:T(4,128)} %bitcast.26, f32[128,3,128]{2,1,0:T(4,128)} %bitcast.27, f32[512,128]{1,0:T(8,128)} %bitcast.28, ...), custom_call_target="tpu_custom_call" | custom-call | tf_op jit(solution)/shard_map/stats/pallas_call | solution.py:438
  17.4 0.0 copy-start.1
  17.4 5.6 %pack.1.src = f32[129,16,128]{2,1,0:T(8,128)} custom-call(s32[8,128]{1,0:T(8,128)} %get-tuple-element.6.meta, s32[128,128]{1,0:T(8,128)} %bitcast.33, f32[49,16384]{1,0:T(8,128)} %attrs.1, f32[3,16384]{1,0:T(4,128)} %means.1, f32[3,16384]{1,0:T(4,128)} %scales.1, f32[4,16384]{1,0:T(4,128)} %quats.1, f32[2,16384]{1,0:T(2,128)} %bitcast.30), custom_call_target="tpu_custom_call" | custom-call | tf_op jit(solution)/shard_map/pack/pallas_call | solution.py:466
  23.0 37.0 %ship.1.buf = f32[4,128,16,128]{3,2,1,0:T(8,128)} custom-call(f32[129,16,128]{2,1,0:T(8,128)} %pack.1.src), custom_call_target="tpu_custom_call" | custom-call | tf_op jit(solution)/shard_map/ship/pallas_call | solution.py:481
  60.0 0.0 copy-done.1
  60.0 0.0 copy-start
  60.0 2.2 %copy-done = f32[4,128,16,128]{3,2,1,0:T(8,128)S(1)} copy-done((f32[4,128,16,128]{3,2,1,0:T(8,128)S(1)}, f32[4,128,16,128]{3,2,1,0:T(8,128)}, u32[]{:S(2)}) %copy-start) | copy-done | bytes 4194328
  62.2 0.0 copy-start.2
  62.2 3.5 %place.1 = f32[61,16384]{1,0:T(8,128)} custom-call(s32[8,128]{1,0:T(8,128)S(1)} %copy-done.1, f32[4,128,16,128]{3,2,1,0:T(8,128)S(1)} %copy-done), custom_call_target="tpu_custom_call" | custom-call | tf_op jit(solution)/shard_map/place/pallas_call | solution.py:492
  65.7 0.5 slice.3
  66.2 0.0 copy-done.2
  66.2 0.7 copy.18
Async XLA Ops:
  17.4 42.6 %copy-start.1 = (s32[8,128]{1,0:T(8,128)S(1)}, s32[8,128]{1,0:T(8,128)}, u32[]{:S(2)}) copy-start(s32[8,128]{1,0:T(8,128)} %get-tuple-element.6.meta) | copy-start | bytes 12292
  60.0 2.2 %copy-start = (f32[4,128,16,128]{3,2,1,0:T(8,128)S(1)}, f32[4,128,16,128]{3,2,1,0:T(8,128)}, u32[]{:S(2)}) copy-start(f32[4,128,16,128]{3,2,1,0:T(8,128)} %ship.1.buf) | copy-start | bytes 12582916
  62.2 4.0 %copy-start.2 = (f32[128,2,128]{2,1,0:T(2,128)S(1)}, f32[128,2,128]{2,1,0:T(2,128)}, u32[]{:S(2)}) copy-start(f32[128,2,128]{2,1,0:T(2,128)} %get-tuple-element.5) | copy-start | bytes 393220

commit v4 on v3

--- a/solution.py
+++ b/solution.py
@@ -58,19 +58,28 @@
 
 
 def stats_kernel(
-    V, S, views, rots, trns, foc, mask, means, scales, quats, grad, vis, peak, meta,
-    cnt, counts, local, halves, merged, whole, total_max,
-    csend, crecv, rsend, rrecv, gsend, grecv,
+    S, views, rots, trns, foc, mask, means, scales, quats, grad, vis, local, meta,
+    cnt, counts, csend, crecv,
 ):
     v, s = lax.axis_index("view"), lax.axis_index("gauss")
     nblk = mask.shape[0]
-    piece = 2 * nblk // V
     cnt[...] = jnp.full((SUB, LANES), jnp.sum(mask[...]), jnp.int32)
     bar = pltpu.get_barrier_semaphore()
     for k in range(1, S):
         pl.semaphore_signal(bar, inc=1, device_id=peer(v, lax.rem(s + k, S)), device_id_type=MESH)
-    for k in range(1, V):
-        pl.semaphore_signal(bar, inc=1, device_id=peer(lax.rem(v + k, V), s), device_id_type=MESH)
+    pl.semaphore_wait(bar, S - 1)
+    tally = []
+    for k in range(1, S):
+        cp = pltpu.make_async_remote_copy(
+            src_ref=cnt,
+            dst_ref=counts.at[k],
+            send_sem=csend.at[k],
+            recv_sem=crecv.at[k],
+            device_id=peer(v, lax.rem(s + k, S)),
+            device_id_type=MESH,
+        )
+        cp.start()
+        tally.append(cp)
 
     step = 2 * SUB
 
@@ -99,51 +108,6 @@
         return carry
 
     lax.fori_loop(0, nblk // step, chunk, 0)
-    pl.semaphore_wait(bar, S + V - 2)
-    copies = []
-    for k in range(1, V):
-        to = lax.rem(v + k, V)
-        rs = pltpu.make_async_remote_copy(
-            src_ref=local.at[pl.ds(pl.multiple_of(to * piece, piece), piece), :],
-            dst_ref=halves.at[k],
-            send_sem=rsend.at[k],
-            recv_sem=rrecv.at[k],
-            device_id=peer(to, s),
-            device_id_type=MESH,
-        )
-        rs.start()
-        copies.append(rs)
-    tally = []
-    for k in range(1, S):
-        cp = pltpu.make_async_remote_copy(
-            src_ref=cnt,
-            dst_ref=counts.at[k],
-            send_sem=csend.at[k],
-            recv_sem=crecv.at[k],
-            device_id=peer(v, lax.rem(s + k, S)),
-            device_id_type=MESH,
-        )
-        cp.start()
-        tally.append(cp)
-    for rs in copies:
-        rs.wait_recv()
-    mine = pl.ds(pl.multiple_of(v * piece, piece), piece)
-    best = local[mine, :]
-    for k in range(1, V):
-        best = jnp.maximum(best, halves[k])
-    merged[...] = best
-    spread = []
-    for k in range(1, V):
-        ag = pltpu.make_async_remote_copy(
-            src_ref=merged,
-            dst_ref=whole.at[k],
-            send_sem=gsend.at[k],
-            recv_sem=grecv.at[k],
-            device_id=peer(lax.rem(v + k, V), s),
-            device_id_type=MESH,
-        )
-        ag.start()
-        spread.append(ag)
     for cp in tally:
         cp.wait_recv()
     lane = lax.broadcasted_iota(jnp.int32, (SUB, LANES), 1)
@@ -159,19 +123,12 @@
         offs = offs + jnp.where(lane > who, b, 0)
         total = total + c
     meta[...] = jnp.where(sub == 0, blocks, jnp.where(sub == 1, offs, total))
-    total_max[mine, :] = best
-    for k in range(1, V):
-        spread[k - 1].wait_recv()
-        who = lax.rem(v + V - k, V)
-        total_max[pl.ds(pl.multiple_of(who * piece, piece), piece), :] = whole[k]
-    for c in range(2):
-        peak[:, c, :] = total_max[pl.ds(c, nblk, stride=2), :]
-    for cp in copies + tally + spread:
+    for cp in tally:
         cp.wait_send()
 
 
 def pack_kernel(
-    V, S, T, per, meta, mask, attrs, means, scales, quats, peak, out,
+    V, S, T, per, meta, mask, attrs, means, scales, quats, out, order,
     x, enc, basev, bases, sem, sem2,
 ):
     v, s = lax.axis_index("view"), lax.axis_index("gauss")
@@ -239,8 +196,7 @@
         @pl.when(tile == ATTR_TILES + 1)
         def _():
             x[j, 0:2, :] = quats[2:4, :]
-            x[j, 3:5, :] = peak[...]
-            x[j, 5:8, :] = jnp.zeros((3, peak.shape[1]), jnp.float32)
+            x[j, 3:8, :] = jnp.zeros((5, quats.shape[1]), jnp.float32)
             pltpu.make_async_copy(
                 attrs.at[pl.ds(ATTR_TILES * SUB, 1), :], x.at[j, pl.ds(2, 1), :], sem.at[j]
             ).wait()
@@ -250,6 +206,7 @@
             pltpu.make_async_copy(attrs.at[pl.ds(0, SUB), :], x.at[j], sem.at[j]).wait()
 
     out[...] = jnp.zeros_like(out)
+    order[...] = jnp.full_like(order, -1)
     scal.wait()
     offset = meta[1, s]
     row = lax.broadcasted_iota(jnp.int32, (SUB, LANES), 1)
@@ -269,19 +226,24 @@
         where = spot(d)
         cols = pl.ds(pl.multiple_of(b * LANES, LANES), LANES)
         full = bases[1, b] >= (d + 1) * LANES
+        gid = b * LANES + idx
+        keep = jnp.where(low, gid, cur[T])
+        order[pl.ds(where, 1), :] = keep[0:1]
+        last = jnp.where(full, jnp.where(high, gid, -1), keep)
         nxt = []
         for j in range(T):
             g = jnp.take_along_axis(x[j, :, cols], idx, axis=1)
             keep = jnp.where(low, g, cur[j])
             out[where, j * SUB:(j + 1) * SUB, :] = keep
             nxt.append(jnp.where(full, jnp.where(high, g, 0.0), keep))
-        return tuple(nxt)
+        return tuple(nxt) + (last,)
 
     zero = jnp.zeros((SUB, LANES), jnp.float32)
-    cur = lax.fori_loop(0, nblk, move, (zero,) * T, unroll=8)
+    cur = lax.fori_loop(0, nblk, move, (zero,) * T + (jnp.full((SUB, LANES), -1, jnp.int32),), unroll=8)
     end = lax.div(bases[1, nblk - 1], LANES)
     for j in range(T):
         out[spot(end), j * SUB:(j + 1) * SUB, :] = cur[j]
+    order[pl.ds(spot(end), 1), :] = cur[T][0:1]
 
 
 def pair(s, k, S):
@@ -295,88 +257,176 @@
     return t, t
 
 
-def ship_kernel(V, S, per, src, buf, gsend, vsend, csend, recv, lsem):
+def ship_kernel(
+    V, S, T, per, src, local, order, buf, peak,
+    halves, merged, whole, best, tile,
+    rsend, rrecv, msend, mrecv, gsend, vsend, csend, recv, lsem,
+):
     v, s = lax.axis_index("view"), lax.axis_index("gauss")
     core = lax.rem(v, 2)
     mate = v + 1 - 2 * core
     X = V // 2
+    nblk = peak.shape[0]
+    piece = 2 * nblk // V
     bar = pltpu.get_barrier_semaphore()
     for k in range(1, S):
         pl.semaphore_signal(bar, inc=1, device_id=peer(v, lax.rem(s + k, S)), device_id_type=MESH)
-    for q in range(1, X):
-        pl.semaphore_signal(
-            bar, inc=1, device_id=peer(lax.rem(v + 2 * q, V), s), device_id_type=MESH
-        )
-    pl.semaphore_signal(bar, inc=1, device_id=peer(mate, s), device_id_type=MESH)
-    pl.semaphore_wait(bar, S - 1 + X)
+    for k in range(1, V):
+        pl.semaphore_signal(bar, inc=1, device_id=peer(lax.rem(v + k, V), s), device_id_type=MESH)
+    pl.semaphore_wait(bar, S + V - 2)
+    started = []
+
+    def go(copy):
+        copy.start()
+        started.append(copy)
 
     def part(i):
         return pl.ds(i * per, per)
 
-    def far(k):
+    def row(j):
+        return pl.ds(j * SUB, SUB)
+
+    def mine(i, j):
+        return tile.at[part(i)] if j == T - 1 else src.at[part(i), row(j), :]
+
+    def remote(ref, owner, frm, j, send, sem, to):
+        return pltpu.make_async_remote_copy(
+            src_ref=ref, dst_ref=buf.at[owner, part(frm), row(j), :],
+            send_sem=send, recv_sem=sem, device_id=to, device_id_type=MESH,
+        )
+
+    def far(k, j):
         to = pair(s, k, S)[0]
-        return pltpu.make_async_remote_copy(
-            src_ref=src.at[part(to)], dst_ref=buf.at[v, part(s)],
-            send_sem=gsend.at[k], recv_sem=recv.at[0, k],
-            device_id=peer(v, to), device_id_type=MESH,
-        )
-
-    def at(k, q):
+        return remote(mine(to, j), v, s, j, gsend.at[k, j], recv.at[0, k, j], peer(v, to))
+
+    def at(k, q, j):
         owner = lax.rem(v + V - 2 * q, V)
         frm = pair(s, k, S)[1]
         if k == 0 and q == 0:
-            return src.at[part(s)], owner, frm
-        return buf.at[owner, part(frm)], owner, frm
-
-    def across(k, q):
-        ref, _, frm = at(k, 0)
-        return pltpu.make_async_remote_copy(
-            src_ref=ref, dst_ref=buf.at[v, part(frm)],
-            send_sem=vsend.at[q, k], recv_sem=recv.at[q, k],
-            device_id=peer(lax.rem(v + 2 * q, V), s), device_id_type=MESH,
+            return mine(s, j), owner, frm
+        return buf.at[owner, part(frm), row(j), :], owner, frm
+
+    def across(k, q, j):
+        ref, _, frm = at(k, 0, j)
+        to = peer(lax.rem(v + 2 * q, V), s)
+        return remote(ref, v, frm, j, vsend.at[q, k, j], recv.at[q, k, j], to)
+
+    def beside(k, q, j):
+        ref, owner, frm = at(k, q, j)
+        return remote(
+            ref, owner, frm, j, csend.at[q, k, j], recv.at[X + q, k, j], peer(mate, s)
         )
 
-    def beside(k, q):
-        ref, owner, frm = at(k, q)
-        return pltpu.make_async_remote_copy(
-            src_ref=ref, dst_ref=buf.at[owner, part(frm)],
-            send_sem=csend.at[q, k], recv_sem=recv.at[X + q, k],
-            device_id=peer(mate, s), device_id_type=MESH,
-        )
-
-    started = []
-
-    def go(copy):
-        copy.start()
-        started.append(copy)
-
-    fars = {k: far(k) for k in range(1, S)}
+    def forward(k, j):
+        if k:
+            far(k, j).wait_recv()
+        for q in range(1, X):
+            go(across(k, q, j))
+        go(beside(k, 0, j))
+
+    def relay(k, j):
+        for q in range(1, X):
+            across(k, q, j).wait_recv()
+            go(beside(k, q, j))
+
+    def lot(i):
+        return pl.ds(pl.multiple_of(i * piece, piece), piece)
+
+    halve = []
+    for k in range(1, V):
+        to = lax.rem(v + k, V)
+        halve.append(pltpu.make_async_remote_copy(
+            src_ref=local.at[lot(to), :], dst_ref=halves.at[k],
+            send_sem=rsend.at[k], recv_sem=rrecv.at[k],
+            device_id=peer(to, s), device_id_type=MESH,
+        ))
+        go(halve[-1])
+    for j in range(T - 1):
+        for k in range(1, S):
+            go(far(k, j))
+        forward(0, j)
+    tile[...] = src[0:S * per, (T - 1) * SUB:T * SUB, :]
+    for copy in halve:
+        copy.wait_recv()
+    top = local[lot(v), :]
+    for k in range(1, V):
+        top = jnp.maximum(top, halves[k])
+    merged[...] = top
+    best[lot(v), :] = top
+    spread = []
+    for k in range(1, V):
+        spread.append(pltpu.make_async_remote_copy(
+            src_ref=merged, dst_ref=whole.at[k],
+            send_sem=msend.at[k], recv_sem=mrecv.at[k],
+            device_id=peer(lax.rem(v + k, V), s), device_id_type=MESH,
+        ))
+        go(spread[-1])
+    for j in range(T - 1):
+        forward(1, j)
+    for k in range(1, V):
+        spread[k - 1].wait_recv()
+        best[lot(lax.rem(v + V - k, V)), :] = whole[k]
+    for c in range(2):
+        peak[:, c, :] = best[pl.ds(c, nblk, stride=2), :]
+
+    @pl.when(v * T + T == TILES)
+    def _():
+        group = 4 * SUB
+
+        def fetch(i, carry):
+            rows = pl.ds(pl.multiple_of(i * group, group), group)
+            idx = order[rows, :]
+            blk, lane = idx >> 7, idx & (LANES - 1)
+
+            def look(b, acc):
+                hit = blk == b
+                return tuple(
+                    jnp.where(
+                        hit,
+                        jnp.take_along_axis(
+                            jnp.broadcast_to(best[pl.ds(2 * b + c, 1), :], idx.shape), lane, axis=1
+                        ),
+                        acc[c],
+                    )
+                    for c in range(2)
+                )
+
+            zero = jnp.zeros(idx.shape, jnp.float32)
+            acc = lax.fori_loop(0, nblk, look, (zero, zero), unroll=4)
+            tile[rows, 3, :] = acc[0]
+            tile[rows, 4, :] = acc[1]
+            return carry
+
+        lax.fori_loop(0, S * per // group, fetch, 0)
+
     for k in range(1, S):
-        go(fars[k])
-    for q in range(1, X):
-        go(across(0, q))
-    go(beside(0, 0))
-    own = pltpu.make_async_copy(src.at[part(s)], buf.at[v, part(s)], lsem)
-    own.start()
-    for k in range(S):
-        if k:
-            fars[k].wait_recv()
-            for q in range(1, X):
-                go(across(k, q))
-            go(beside(k, 0))
-        if k:
-            for q in range(1, X):
-                across(k - 1, q).wait_recv()
-                go(beside(k - 1, q))
-    for q in range(1, X):
-        across(S - 1, q).wait_recv()
-        go(beside(S - 1, q))
-    for k in range(S):
-        for q in range(X):
-            beside(k, q).wait_recv()
+        go(far(k, T - 1))
+    own = []
+    for j in range(T):
+        own.append(pltpu.make_async_copy(mine(s, j), buf.at[v, part(s), row(j), :], lsem.at[j]))
+        own[-1].start()
+    for j in range(T - 1):
+        relay(0, j)
+        for k in range(2, S):
+            forward(k, j)
+            relay(k - 1, j)
+            if k == 2:
+                forward(0, T - 1)
+        relay(S - 1, j)
+    if T == 1:
+        forward(0, T - 1)
+    for k in range(1, S):
+        forward(k, T - 1)
+        relay(k - 1, T - 1)
+    relay(S - 1, T - 1)
+    for j in range(T):
+        for k in range(S):
+            for q in range(X):
+                beside(k, q, j).wait_recv()
     for copy in started:
         copy.wait_send()
-    own.wait()
+    for copy in own:
+        copy.wait()
 
 
 def place_kernel(S, T, per, meta, buf, out):
@@ -435,23 +485,16 @@
 
     dma = pltpu.SemaphoreType.DMA
     piece = 2 * nblk // V
-    peak2, meta = pl.pallas_call(
-        functools.partial(stats_kernel, V, S, views),
+    local, meta = pl.pallas_call(
+        functools.partial(stats_kernel, S, views),
         out_shape=(
-            jax.ShapeDtypeStruct((nblk, 2, LANES), f32),
+            jax.ShapeDtypeStruct((2 * nblk, LANES), f32),
             jax.ShapeDtypeStruct((SUB, LANES), i32),
         ),
         in_specs=[spec(SMEM)] * 3 + [spec(VMEM)] * 6,
         out_specs=(spec(VMEM), spec(VMEM)),
         scratch_shapes=[
-            VMEM((SUB, LANES), i32),
-            VMEM((S, SUB, LANES), i32),
-            VMEM((2 * nblk, LANES), f32),
-            VMEM((V, piece, LANES), f32),
-            VMEM((piece, LANES), f32),
-            VMEM((V, piece, LANES), f32),
-            VMEM((2 * nblk, LANES), f32),
-            dma((S,)), dma((S,)), dma((V,)), dma((V,)), dma((V,)), dma((V,)),
+            VMEM((SUB, LANES), i32), VMEM((S, SUB, LANES), i32), dma((S,)), dma((S,)),
         ],
         compiler_params=pltpu.CompilerParams(collective_id=0, has_side_effects=True),
         name="stats",
@@ -460,14 +503,17 @@
         lines(quats).reshape(-1, LANES), lines(grad_screen).reshape(views, -1, LANES),
         lines(visible).reshape(-1, LANES),
     )
-    peak = jnp.swapaxes(peak2, 0, 1).reshape(2, G)
     total = meta[2, 0]
     R = T * SUB
-    packed = pl.pallas_call(
+    X = V // 2
+    packed, order = pl.pallas_call(
         functools.partial(pack_kernel, V, S, T, per),
-        out_shape=jax.ShapeDtypeStruct((S * per + 1, R, LANES), f32),
-        in_specs=[spec(SMEM), spec(VMEM), spec(pl.ANY)] + [spec(VMEM)] * 4,
-        out_specs=spec(VMEM),
+        out_shape=(
+            jax.ShapeDtypeStruct((S * per + 1, R, LANES), f32),
+            jax.ShapeDtypeStruct((S * per + SUB, LANES), i32),
+        ),
+        in_specs=[spec(SMEM), spec(VMEM), spec(pl.ANY)] + [spec(VMEM)] * 3,
+        out_specs=(spec(VMEM), spec(VMEM)),
         scratch_shapes=[
             VMEM((T, SUB, G), f32),
             VMEM((nblk, LANES), i32),
@@ -476,19 +522,28 @@
             dma((T,)), dma,
         ],
         name="pack",
-    )(meta, mask, attrs, means, scales, quats, peak)
-    X = V // 2
-    buf = pl.pallas_call(
-        functools.partial(ship_kernel, V, S, per),
-        out_shape=jax.ShapeDtypeStruct((V, S * per, R, LANES), f32),
-        in_specs=[spec(VMEM)],
-        out_specs=spec(pl.ANY),
+    )(meta, mask, attrs, means, scales, quats)
+    buf, peak2 = pl.pallas_call(
+        functools.partial(ship_kernel, V, S, T, per),
+        out_shape=(
+            jax.ShapeDtypeStruct((V, S * per, R, LANES), f32),
+            jax.ShapeDtypeStruct((nblk, 2, LANES), f32),
+        ),
+        in_specs=[spec(VMEM)] * 3,
+        out_specs=(spec(pl.ANY), spec(VMEM)),
         scratch_shapes=[
-            dma((S,)), dma((X, S)), dma((X, S)), dma((2 * X, S)), dma,
+            VMEM((V, piece, LANES), f32),
+            VMEM((piece, LANES), f32),
+            VMEM((V, piece, LANES), f32),
+            VMEM((2 * nblk, LANES), f32),
+            VMEM((S * per, SUB, LANES), f32),
+            dma((V,)), dma((V,)), dma((V,)), dma((V,)),
+            dma((S, T)), dma((X, S, T)), dma((X, S, T)), dma((2 * X, S, T)), dma((T,)),
         ],
         compiler_params=pltpu.CompilerParams(collective_id=1, has_side_effects=True),
         name="ship",
-    )(packed)
+    )(packed, local, order)
+    peak = jnp.swapaxes(peak2, 0, 1).reshape(2, G)
     clones = pl.pallas_call(
         functools.partial(place_kernel, S, T, per),
         out_shape=jax.ShapeDtypeStruct((rows, G), f32),

time: 67.2 us -> 82.7 us (1.23)
  Pallas kernels: 61.5 us -> 77.1 us
    pallas_call x3, Pallas kernels: 58 us -> 73.6 us  [the longest x1 54.4 us: body(): pl.pallas_call(functools.partial(ship_kernel, V, S, T, per), out_shape=(j...]
where the time goes in v4:
time: 82.7 us; the launch traced here: 82.4 us
  Pallas kernels  77.1 us (93%)
  local copies, waits for them, and re-layouts  4.65 us (6%)
    pallas_call x1, Pallas kernels, body(): pl.pallas_call(functools.partial(ship_kernel, V, S, T, per), out_shape=(j...  54.4 us
    pallas_call x1, Pallas kernels, body(): pl.pallas_call(functools.partial(stats_kernel, S, views), out_shape=(jax....  13.5 us
    pallas_call x1, Pallas kernels, body(): pl.pallas_call(functools.partial(pack_kernel, V, S, T, per), out_shape=(j...  5.67 us
    unnamed x8, local copies, waits for them, and re-layouts  4.14 us
    pallas_call x1, Pallas kernels, body(): pl.pallas_call(functools.partial(place_kernel, S, T, per), out_shape=jax....  3.48 us

profile of v4, /device:TPU:0, one launch (start us, length us, event | category | flops | bytes accessed | tf_op | source)
XLA Modules:
  0.0 82.4 jit_solution(17385178949004067976)
XLA Ops:
  0.6 1.3 %copy.16.rots = f32[4,3,3]{2,1,0:T(4,128)} copy(f32[4,3,3]{2,0,1:T(4,128)} %param.17) | data formatting | bytes 288 | tf_op args[7]
  1.9 13.5 %stats.1 = (f32[256,128]{1,0:T(8,128)}, s32[8,128]{1,0:T(8,128)}) custom-call(f32[4,3,3]{2,1,0:T(4,128)} %copy.16.rots, f32[4,3]{1,0:T(4,128)} %trns.1, f32[4]{0:T(128)} %foc.1, s32[128,128]{1,0:T(8,128)} %bitcast.30, f32[128,3,128]{2,1,0:T(4,128)} %bitcast.26, f32[128,3,128]{2,1,0:T(4,128)} %bitcast.27, f32[512,128]{1,0:T(8,128)} %bitcast.28, ...), custom_call_target="tpu_custom_call" | custom-call | tf_op jit(solution)/shard_map/stats/pallas_call | solution.py:488
  15.4 0.0 copy-start.1
  15.4 5.7 %pack.1 = (f32[129,16,128]{2,1,0:T(8,128)}, s32[136,128]{1,0:T(8,128)}) custom-call(s32[8,128]{1,0:T(8,128)} %get-tuple-element.9.meta, s32[128,128]{1,0:T(8,128)} %bitcast.31, f32[49,16384]{1,0:T(8,128)} %attrs.1, f32[3,16384]{1,0:T(4,128)} %means.1, f32[3,16384]{1,0:T(4,128)} %scales.1, f32[4,16384]{1,0:T(4,128)} %quats.1), custom_call_target="tpu_custom_call" | custom-call | tf_op jit(solution)/shard_map/pack/pallas_call | solution.py:509
  21.1 54.4 %ship.1 = (f32[4,128,16,128]{3,2,1,0:T(8,128)}, f32[128,2,128]{2,1,0:T(2,128)}) custom-call(f32[129,16,128]{2,1,0:T(8,128)} %get-tuple-element.10.src, f32[256,128]{1,0:T(8,128)} %get-tuple-element.11.local, s32[136,128]{1,0:T(8,128)} %get-tuple-element.12.order), custom_call_target="tpu_custom_call" | custom-call | tf_op jit(solution)/shard_map/ship/pallas_call | solution.py:526
  75.6 0.0 copy-done.1
  75.6 0.0 copy-start
  75.6 2.2 %copy-done = f32[4,128,16,128]{3,2,1,0:T(8,128)S(1)} copy-done((f32[4,128,16,128]{3,2,1,0:T(8,128)S(1)}, f32[4,128,16,128]{3,2,1,0:T(8,128)}, u32[]{:S(2)}) %copy-start) | copy-done | bytes 4194328
  77.8 0.0 copy-start.2
  77.8 3.5 %place.1 = f32[61,16384]{1,0:T(8,128)} custom-call(s32[8,128]{1,0:T(8,128)S(1)} %copy-done.1, f32[4,128,16,128]{3,2,1,0:T(8,128)S(1)} %copy-done), custom_call_target="tpu_custom_call" | custom-call | tf_op jit(solution)/shard_map/place/pallas_call | solution.py:547
  81.2 0.5 slice.3
  81.8 0.0 copy-done.2
  81.8 0.7 copy.18
Async XLA Ops:
  15.4 60.1 %copy-start.1 = (s32[8,128]{1,0:T(8,128)S(1)}, s32[8,128]{1,0:T(8,128)}, u32[]{:S(2)}) copy-start(s32[8,128]{1,0:T(8,128)} %get-tuple-element.9.meta) | copy-start | bytes 12292
  75.6 2.2 %copy-start = (f32[4,128,16,128]{3,2,1,0:T(8,128)S(1)}, f32[4,128,16,128]{3,2,1,0:T(8,128)}, u32[]{:S(2)}) copy-start(f32[4,128,16,128]{3,2,1,0:T(8,128)} %get-tuple-element.14.buf) | copy-start | bytes 12582916
  77.8 4.0 %copy-start.2 = (f32[128,2,128]{2,1,0:T(2,128)S(1)}, f32[128,2,128]{2,1,0:T(2,128)}, u32[]{:S(2)}) copy-start(f32[128,2,128]{2,1,0:T(2,128)} %get-tuple-element.13) | copy-start | bytes 393220
